TPU v7x, 256 devices: a whole 4x4x8 slice. The times are simulated.
256 devices in a mesh: rows: 32 (over x, z), tensor: 2 (over core), groups: 4 (over y).
Axes of the slice: x: 4, y: 4, z: 8, core: 2. Of those that a mesh axis runs over, the one named last changes fastest.
Arguments:
- effects: float32 [32768, 1024], P(('groups', 'rows'), 'tensor'), parts along dimension 0, may hold values from -8 to 8
Outputs:
- basis: float32 [32768, 1024], P(('groups', 'rows'), 'tensor'), parts along dimension 0
- triangle: float32 [4096, 1024], P('groups', 'tensor'), parts along dimension 0
There are 4 independent parts, one for each index of `groups`. A program takes and returns all parts, laid end to end along the dimension named above; each array names one. Nothing has to cross between parts.
All inputs are finite; a program needn't handle non-finite values.
Results may differ from a plain program's by a relative error of at most 0.000075.
Values sent between devices are 32-bit elements; how exact they have to be, the bound alone decides.
A program may use at most 64 MiB of HBM per device.

v0:
```python
import jax
import jax.numpy as jnp
from jax import lax
from jax.sharding import PartitionSpec as P


def in_order(parts, dim):
    dims = list(parts.shape[1:])
    dims[dim] *= parts.shape[0]
    return jnp.moveaxis(parts, 0, dim).reshape(dims)


def from_everyone(value, axis):
    size = lax.axis_size(axis)
    return lax.all_to_all(
        jnp.broadcast_to(value[None], (size, *value.shape)), axis, 0, 0, tiled=True
    )


def gather_directly(value, axis, dim):
    return in_order(from_everyone(value, axis), dim)


def shards(effects):
    whole = gather_directly(effects, "tensor", 1)
    width = effects.shape[1]
    local_gram = jnp.dot(
        whole.T, whole, precision=lax.Precision.HIGHEST, preferred_element_type=jnp.float32
    )
    gram = lax.psum(local_gram, "rows")
    lower = jnp.linalg.cholesky(gram)
    total = effects.shape[0] * lax.axis_size("rows")
    scale = jnp.sqrt(jnp.float32(total))
    full_width = whole.shape[1]
    start = lax.axis_index("tensor") * width
    position = lax.broadcasted_iota(jnp.int32, (full_width, width), 0)
    column_id = lax.broadcasted_iota(jnp.int32, (full_width, width), 1) + start
    identity_cols = jnp.where(position == column_id, jnp.float32(1.0), jnp.float32(0.0))
    inverse_cols = lax.linalg.triangular_solve(
        lower, identity_cols, left_side=True, lower=True, transpose_a=True
    )
    own_solved = jnp.dot(
        whole, inverse_cols, precision=lax.Precision.HIGHEST, preferred_element_type=jnp.float32
    )
    basis = own_solved * scale
    own_lower = lax.dynamic_slice_in_dim(lower, start, width, 0)
    triangle = own_lower.T / scale
    return (basis, triangle)


def solution(mesh):
    in_specs = (P(("groups", "rows"), "tensor"),)
    out_specs = (P(("groups", "rows"), "tensor"), P("groups", "tensor"))
    return jax.shard_map(shards, mesh=mesh, in_specs=in_specs, out_specs=out_specs, check_vma=False)
```

profile of v0, /device:TPU:1, one launch (start us, length us, event | category | flops | bytes accessed | tf_op | source)
XLA Modules:
  0.0 542.9 jit_solution(1766402507569744709)
XLA Ops:
  8.5 7.4 %all_to_all.5 = f32[2,256,512]{1,2,0:T(8,128)S(1)} all-to-all(f32[2,256,512]{1,2,0:T(8,128)S(1)} %broadcast_in_dim.16), channel_id=1, replica_groups=mesh['rows'=32,'tensor'=2,'groups'=4] {'tensor'}, dimensions={0} | all-to-all | bytes 2097152 | tf_op jit(solution)/shard_map/all_to_all | solution.py:15
  15.9 5.1 fusion.65
  22.8 160.6 %all-reduce.3.cloned.1.call-done = f32[1024,1024]{0,1:T(8,128)} async-done(((f32[1024,1024]{0,1:T(8,128)}), f32[1024,1024]{0,1:T(8,128)}) %all-reduce.3.cloned.1.call-update) | async-done | bytes 4194320 | tf_op jit(solution)/shard_map/psum | solution.py:30
  183.4 5.5 %copy.9 = f32[1024,1024]{1,0:T(8,128)} copy(f32[1024,1024]{0,1:T(8,128)} %all-reduce.3.cloned.1.call-done) | data formatting | bytes 8388608 | tf_op jit(solution)/shard_map/psum | solution.py:30
  188.9 4.4 fusion
  195.3 11.7 %cholesky.223 = f32[128,128]{1,0:T(8,128)S(1)} custom-call(f32[128,128]{1,0:T(8,128)S(1)} %cholesky.580), custom_call_target="Cholesky" | custom-call | tf_op jit(solution)/shard_map/jit(cholesky)/cholesky | solution.py:31
  207.0 9.8 %custom-call.62 = f32[1,128,128]{1,2,0:T(8,128)S(1)} custom-call(f32[1,128,128]{2,1,0:T(8,128)S(1)} %get-tuple-element.47), custom_call_target="InvertDiagBlocksLowerTriangular" | custom-call | tf_op jit(solution)/shard_map/jit(cholesky)/cholesky | solution.py:31
  223.3 11.9 %cholesky.244 = f32[128,128]{1,0:T(8,128)S(1)} custom-call(f32[128,128]{1,0:T(8,128)S(1)} %cholesky.584), custom_call_target="Cholesky" | custom-call | tf_op jit(solution)/shard_map/jit(cholesky)/cholesky | solution.py:31
  235.8 9.8 %custom-call.63 = f32[1,128,128]{1,2,0:T(8,128)S(1)} custom-call(f32[1,128,128]{2,1,0:T(8,128)S(1)} %get-tuple-element.44), custom_call_target="InvertDiagBlocksLowerTriangular" | custom-call | tf_op jit(solution)/shard_map/jit(cholesky)/cholesky | solution.py:31
  249.0 11.7 %cholesky.468 = f32[128,128]{1,0:T(8,128)S(1)} custom-call(f32[128,128]{1,0:T(8,128)S(1)} %cholesky.589), custom_call_target="Cholesky" | custom-call | tf_op jit(solution)/shard_map/jit(cholesky)/cholesky | solution.py:31
  261.9 9.8 %custom-call.64 = f32[1,128,128]{1,2,0:T(8,128)S(1)} custom-call(f32[1,128,128]{2,1,0:T(8,128)S(1)} %get-tuple-element.41), custom_call_target="InvertDiagBlocksLowerTriangular" | custom-call | tf_op jit(solution)/shard_map/jit(cholesky)/cholesky | solution.py:31
  275.3 12.1 %cholesky.487 = f32[128,128]{1,0:T(8,128)S(1)} custom-call(f32[128,128]{1,0:T(8,128)S(1)} %cholesky.594), custom_call_target="Cholesky" | custom-call | tf_op jit(solution)/shard_map/jit(cholesky)/cholesky | solution.py:31
  288.7 9.8 %custom-call.65 = f32[1,128,128]{1,2,0:T(8,128)S(1)} custom-call(f32[1,128,128]{2,1,0:T(8,128)S(1)} %get-tuple-element.38), custom_call_target="InvertDiagBlocksLowerTriangular" | custom-call | tf_op jit(solution)/shard_map/jit(cholesky)/cholesky | solution.py:31
  302.0 11.7 %cholesky.506 = f32[128,128]{1,0:T(8,128)S(1)} custom-call(f32[128,128]{1,0:T(8,128)S(1)} %cholesky.599), custom_call_target="Cholesky" | custom-call | tf_op jit(solution)/shard_map/jit(cholesky)/cholesky | solution.py:31
  315.0 9.9 %custom-call.66 = f32[1,128,128]{1,2,0:T(8,128)S(1)} custom-call(f32[1,128,128]{2,1,0:T(8,128)S(1)} %get-tuple-element.35), custom_call_target="InvertDiagBlocksLowerTriangular" | custom-call | tf_op jit(solution)/shard_map/jit(cholesky)/cholesky | solution.py:31
  328.3 11.7 %cholesky.526 = f32[128,128]{1,0:T(8,128)S(1)} custom-call(f32[128,128]{1,0:T(8,128)S(1)} %cholesky.604), custom_call_target="Cholesky" | custom-call | tf_op jit(solution)/shard_map/jit(cholesky)/cholesky | solution.py:31
  341.3 9.8 %custom-call.67 = f32[1,128,128]{1,2,0:T(8,128)S(1)} custom-call(f32[1,128,128]{2,1,0:T(8,128)S(1)} %get-tuple-element.32), custom_call_target="InvertDiagBlocksLowerTriangular" | custom-call | tf_op jit(solution)/shard_map/jit(cholesky)/cholesky | solution.py:31
  354.1 11.9 %cholesky.546 = f32[128,128]{1,0:T(8,128)S(1)} custom-call(f32[128,128]{1,0:T(8,128)S(1)} %cholesky.609), custom_call_target="Cholesky" | custom-call | tf_op jit(solution)/shard_map/jit(cholesky)/cholesky | solution.py:31
  367.3 9.8 %custom-call.68 = f32[1,128,128]{1,2,0:T(8,128)S(1)} custom-call(f32[1,128,128]{2,1,0:T(8,128)S(1)} %get-tuple-element.29), custom_call_target="InvertDiagBlocksLowerTriangular" | custom-call | tf_op jit(solution)/shard_map/jit(cholesky)/cholesky | solution.py:31
  379.7 11.7 %cholesky.564 = f32[128,128]{1,0:T(8,128)S(1)} custom-call(f32[128,128]{1,0:T(8,128)S(1)} %convolution_subtract_fusion.13), custom_call_target="Cholesky" | custom-call | tf_op jit(solution)/shard_map/jit(cholesky)/cholesky | solution.py:31
  398.3 4.8 fusion.1
  405.2 27.8 %while.1 = (s32[]{:T(128)}, f32[1024,1024]{1,0:T(8,128)}, s32[8,2]{0,1:T(2,128)S(1)}, f32[8,128,128]{2,1,0:T(8,128)}, s32[]{:T(128)}) while((s32[]{:T(128)}, f32[1024,1024]{1,0:T(8,128)}, s32[8,2]{0,1:T(2,128)S(1)}, f32[8,128,128]{2,1,0:T(8,128)}, s32[]{:T(128)}) %tuple.45), condition=%wide.while_cond, body=%wide.while_body.sunk | while | flops 2 | bytes 132205 | solution.py:39
  405.8 2.9 bitcast_dynamic-update-slice_fusion.2
  409.3 2.9 bitcast_dynamic-update-slice_fusion.2
  412.8 2.9 bitcast_dynamic-update-slice_fusion.2
  416.2 2.9 bitcast_dynamic-update-slice_fusion.2
  419.7 2.9 bitcast_dynamic-update-slice_fusion.2
  423.2 2.9 bitcast_dynamic-update-slice_fusion.2
  426.7 2.9 bitcast_dynamic-update-slice_fusion.2
  430.1 2.8 bitcast_dynamic-update-slice_fusion.2
  432.9 80.3 %custom-call.69 = f32[8,128,128]{1,2,0:T(8,128)} custom-call(f32[8,128,128]{2,1,0:T(8,128)} %get-tuple-element.9), custom_call_target="InvertDiagBlocksLowerTriangular" | custom-call | tf_op jit(solution)/shard_map/triangular_solve | solution.py:39
  531.1 3.5 fusion.3
  (108 shorter events, 65.3 us)
Async XLA Ops:
  7.2 176.2 %all-reduce.3.cloned.1.call-start = ((), (), s32[]{:S(2)}) async-start(), calls=%async_computation.1 | async-start | bytes 8388608 | tf_op jit(solution)/shard_map/psum | solution.py:30
  193.3 1.9 copy-start
  405.1 112.1 %copy-start.1 = (f32[1024,512]{1,0:T(8,128)S(1)}, f32[1024,512]{1,0:T(8,128)}, u32[]{:S(2)}) copy-start(f32[1024,512]{1,0:T(8,128)} %fusion.2) | copy-start | bytes 6291460
  513.2 5.4 copy-start.2
Sparse Core Ops, SparseCore 0:
  21.2 162.1 all-reduce.2
where the time goes:
time: 549 us; the launch traced here: 543 us
  other arithmetic  264 us (48%)
  waiting for transfers between devices  161 us (29%)
  matrix products  48.8 us (9%)
  local copies, waits for them, and re-layouts  42.3 us (8%)
  between operations  19.9 us (4%)
  blocking collectives  7.4 us (1%)
    another operation x30, other arithmetic, shards(): lower = jnp.linalg.cholesky(gram)  172 us
    psum x1, waiting for transfers between devices, shards(): gram = lax.psum(local_gram, 'rows')  161 us
    another operation x3, other arithmetic, shards(): lax.linalg.triangular_solve(lower, identity_cols, left_side=True, lower=T...  85.1 us
    another operation x24, local copies, waits for them, and re-layouts  27.8 us
    another operation x14, matrix products, shards(): lower = jnp.linalg.cholesky(gram)  23.1 us
    another operation x15, matrix products, shards(): lax.linalg.triangular_solve(lower, identity_cols, left_side=True, lower=T...  17.1 us
  transfers between devices with their start and end apart: 1, of which 1 were waited for; matrix products, arithmetic and copies ran while one was open for 0% of the time, Pallas kernels for 0%

commit v1 on v0

v1 whole, which is shorter than its diff:
```python
import jax
import jax.numpy as jnp
from jax import lax
from jax.experimental import pallas as pl
from jax.experimental.pallas import tpu as pltpu
from jax.sharding import PartitionSpec as P

f32 = jnp.float32
bf16 = jnp.bfloat16
BLOCK = 128
BASE = 32


def split3(x):
    high = x.astype(bf16)
    rest = x - high.astype(f32)
    middle = rest.astype(bf16)
    return high, middle, (rest - middle.astype(f32)).astype(bf16)


def left(parts, dim):
    h, m, l = parts
    return jnp.concatenate([h, h, m, h, m, l], dim)


def right(parts, dim):
    h, m, l = parts
    return jnp.concatenate([h, m, h, l, m, h], dim)


def dot_over(a, b, dim):
    return lax.dot_general(a, b, (((dim,), (dim,)), ((), ())), preferred_element_type=f32)


def eliminate(rows, offset):
    tiles = BASE // 8
    cols = [
        [
            jnp.broadcast_to(rows[8 * t : 8 * t + 8, offset + j : offset + j + 1], (8, BLOCK))
            for t in range(tiles)
        ]
        for j in range(BASE)
    ]
    panel = [
        [rows[8 * t : 8 * t + 8, BLOCK * c : BLOCK * (c + 1)] for c in range(2)]
        for t in range(tiles)
    ]
    row = lax.broadcasted_iota(jnp.int32, (8, BLOCK), 0)
    scales = [jnp.zeros((8, BLOCK), f32) for _ in range(tiles)]
    for j in range(BASE):
        t0, r = divmod(j, 8)
        inv = lax.rsqrt(jnp.broadcast_to(cols[j][t0][r : r + 1], (8, BLOCK)))
        scales[t0] = jnp.where(row == r, inv, scales[t0])
        column = [cols[j][t] * inv for t in range(t0, tiles)]
        below = [jnp.where(row > r, column[0], 0.0)] + column[1:]
        pivot = [jnp.broadcast_to(panel[t0][c][r : r + 1], (8, BLOCK)) * inv for c in range(2)]
        for t in range(t0, tiles):
            for c in range(2):
                panel[t][c] = panel[t][c] - below[t - t0] * pivot[c]
        for j2 in range(j + 1, BASE):
            t2, r2 = divmod(j2, 8)
            factor = jnp.broadcast_to(column[t2 - t0][r2 : r2 + 1], (8, BLOCK))
            for t in range(t2, tiles):
                cols[j2][t] = cols[j2][t] - column[t - t0] * factor
    return jnp.concatenate(
        [jnp.concatenate([panel[t][c] * scales[t] for c in range(2)], 1) for t in range(tiles)], 0
    )


def factor_block(block):
    shape = (BLOCK, BLOCK)
    row = lax.broadcasted_iota(jnp.int32, shape, 0)
    col = lax.broadcasted_iota(jnp.int32, shape, 1)
    rest = jnp.concatenate([block, jnp.where(row == col, 1.0, 0.0).astype(f32)], 1)
    done = []
    for s in range(0, BLOCK, BASE):
        rows = eliminate(rest[:BASE], s)
        at = lax.broadcasted_iota(jnp.int32, rows.shape, 1)
        diag = lax.broadcasted_iota(jnp.int32, rows.shape, 0) + s
        rows = jnp.where(at < jnp.minimum(diag, BLOCK), 0.0, rows)
        done.append(rows)
        if s + BASE < BLOCK:
            update = dot_over(left(split3(rows[:, :BLOCK]), 0), right(split3(rows), 0), 0)
            rest = rest[BASE:] - update[s + BASE :]
    return jnp.concatenate(done, 0)


def factor_kernel(gram_ref, rows_ref, solved_ref, upper_ref, work, lhs, rhs):
    n = gram_ref.shape[0]
    full = n + rows_ref.shape[0]
    work[:n] = gram_ref[...]
    work[n:] = rows_ref[...]
    for c0 in range(0, n, BLOCK):
        c1 = c0 + BLOCK
        if c0:
            upper_ref[c0:c1, :c0] = jnp.zeros((BLOCK, c0), f32)
        factored = factor_block(work[c0:c1, c0:c1])
        upper_ref[c0:c1, c0:c1] = factored[:, :BLOCK]
        inverse = right(split3(factored[:, BLOCK:]), 1)
        for r in range(c1, full, BLOCK):
            solved = dot_over(left(split3(work[r : r + BLOCK, c0:c1]), 1), inverse, 1)
            parts = split3(solved)
            lhs[r : r + BLOCK] = left(parts, 1)
            if r >= n:
                solved_ref[r - n : r - n + BLOCK, c0:c1] = solved
            else:
                upper_ref[c0:c1, r : r + BLOCK] = solved.T
                rhs[r : r + BLOCK] = right(parts, 1)
        j = c1
        while j < n:
            width = BLOCK if (j // BLOCK) % 2 else min(2 * BLOCK, n - j)
            against = rhs[j : j + width]
            for r in range(j, full, 2 * BLOCK):
                h = min(2 * BLOCK, full - r)
                work[r : r + h, j : j + width] -= dot_over(lhs[r : r + h], against, 1)
            j += width


def factor_and_solve(gram, rows):
    n, m = gram.shape[0], rows.shape[0]
    return pl.pallas_call(
        factor_kernel,
        out_shape=[jax.ShapeDtypeStruct((m, n), f32), jax.ShapeDtypeStruct((n, n), f32)],
        scratch_shapes=[
            pltpu.VMEM((n + m, n), f32),
            pltpu.VMEM((n + m, 6 * BLOCK), bf16),
            pltpu.VMEM((n, 6 * BLOCK), bf16),
        ],
        compiler_params=pltpu.CompilerParams(vmem_limit_bytes=60 * 2**20),
    )(gram, rows)


def in_order(parts, dim):
    dims = list(parts.shape[1:])
    dims[dim] *= parts.shape[0]
    return jnp.moveaxis(parts, 0, dim).reshape(dims)


def from_everyone(value, axis):
    size = lax.axis_size(axis)
    return lax.all_to_all(
        jnp.broadcast_to(value[None], (size, *value.shape)), axis, 0, 0, tiled=True
    )


def shards(effects):
    whole = in_order(from_everyone(effects, "tensor"), 1)
    width = effects.shape[1]
    local_gram = jnp.dot(
        whole.T, whole, precision=lax.Precision.HIGHEST, preferred_element_type=jnp.float32
    )
    gram = lax.psum(local_gram, "rows")
    solved, upper = factor_and_solve(gram, whole)
    total = effects.shape[0] * lax.axis_size("rows")
    scale = jnp.sqrt(jnp.float32(total))
    start = lax.axis_index("tensor") * width
    basis = lax.dynamic_slice_in_dim(solved, start, width, 1) * scale
    triangle = lax.dynamic_slice_in_dim(upper, start, width, 1) / scale
    return (basis, triangle)


def solution(mesh):
    in_specs = (P(("groups", "rows"), "tensor"),)
    out_specs = (P(("groups", "rows"), "tensor"), P("groups", "tensor"))
    return jax.shard_map(shards, mesh=mesh, in_specs=in_specs, out_specs=out_specs, check_vma=False)
```

time: 549 us -> 233 us (0.42)
  other arithmetic: 264 us -> 5.04 us
  matrix products: 48.8 us -> 5.06 us
  local copies, waits for them, and re-layouts: 42.3 us -> 1.26 us
  Pallas kernels: 0 us -> 34.9 us
  between operations: 19.9 us -> 14.1 us
    another operation x33 -> x0, other arithmetic: 257 us -> none  [the longest x30 172 us: shards(): lower = jnp.linalg.cholesky(gram)]
    another operation x29 -> x0, matrix products: 40.2 us -> none  [the longest x14 23.1 us: shards(): lower = jnp.linalg.cholesky(gram)]
    pallas_call x0 -> x1, Pallas kernels: none -> 34.9 us  [factor_and_solve(): pl.pallas_call(factor_kernel, out_shape=[jax.ShapeDtypeStruct((m, n), f32...]
    another operation x37 -> x0, local copies, waits for them, and re-layouts: 30.4 us -> none
    unnamed x27 -> x2, local copies, waits for them, and re-layouts: 6.33 us -> 0.01 us
    psum x1 -> x0, local copies, waits for them, and re-layouts: 5.49 us -> none  [shards(): gram = lax.psum(local_gram, 'rows')]
where the time goes in v1:
time: 233 us; the launch traced here: 230 us
  waiting for transfers between devices  162 us (70%)
  Pallas kernels  34.9 us (15%)
  between operations  14.1 us (6%)
  blocking collectives  7.4 us (3%)
  matrix products  5.06 us (2%)
  other arithmetic  5.04 us (2%)
    psum x1, waiting for transfers between devices, shards(): gram = lax.psum(local_gram, 'rows')  162 us
    pallas_call x1, Pallas kernels, factor_and_solve(): pl.pallas_call(factor_kernel, out_shape=[jax.ShapeDtypeStruct((m, n), f32...  34.9 us
    all_to_all x1, blocking collectives, from_everyone(): lax.all_to_all(jnp.broadcast_to(value[None], (size, *value.shape)), axis,...  7.4 us
    dot_general x1, matrix products, shards(): jnp.dot(whole.T, whole, precision=lax.Precision.HIGHEST, preferred_elemen...  5.06 us
  transfers between devices with their start and end apart: 1, of which 1 were waited for; matrix products, arithmetic and copies ran while one was open for 0% of the time, Pallas kernels for 0%

profile of v1, /device:TPU:1, one launch (start us, length us, event | category | flops | bytes accessed | tf_op | source)
XLA Modules:
  0.0 230.3 jit_solution(6293068686381398793)
XLA Ops:
  7.2 0.0 all-reduce.2.cloned.1.call-start
  7.2 1.2 broadcast_in_dim.2
  8.4 7.4 %all_to_all.5 = f32[2,256,512]{2,1,0:T(8,128)S(1)} all-to-all(f32[2,256,512]{2,1,0:T(8,128)S(1)} %broadcast_in_dim.2), channel_id=1, replica_groups=mesh['rows'=32,'tensor'=2,'groups'=4] {'tensor'}, dimensions={0} | all-to-all | bytes 2097152 | tf_op jit(solution)/shard_map/all_to_all | solution.py:141
  15.8 0.1 copy.4
  15.9 0.0 copy-start
  15.9 5.1 %fusion = f32[1024,1024]{1,0:T(8,128)} fusion(f32[256,1024]{1,0:T(8,128)S(1)} %bitcast.5), kind=kOutput, calls=%fused_computation.2 | convolution fusion | flops 3221225472 | bytes 5242880 | tf_op jit(solution)/shard_map/dot_general | solution.py:149
  21.0 0.0 all-reduce.2.cloned.1.call-update
  21.0 0.0 copy-done
  21.0 162.4 %all-reduce.2.cloned.1.call-done.gram_ref = f32[1024,1024]{1,0:T(8,128)} async-done(((f32[1024,1024]{1,0:T(8,128)}), f32[1024,1024]{1,0:T(8,128)}) %all-reduce.2.cloned.1.call-update) | async-done | bytes 4194320 | tf_op jit(solution)/shard_map/psum | solution.py:152
  183.4 34.9 %shard_map.30 = (f32[256,1024]{1,0:T(8,128)}, f32[1024,1024]{1,0:T(8,128)}) custom-call(f32[1024,1024]{1,0:T(8,128)} %all-reduce.2.cloned.1.call-done.gram_ref, f32[256,1024]{1,0:T(8,128)} %bitcast.6), custom_call_target="tpu_custom_call" | custom-call | tf_op jit(solution)/shard_map/pallas_call | solution.py:121
  218.4 1.9 dynamic-slice_multiply_fusion.1
  220.3 3.2 %dynamic-slice_multiply_fusion = f32[1024,512]{1,0:T(8,128)} fusion(f32[1024,1024]{1,0:T(8,128)} %get-tuple-element.5, s32[]{:T(128)S(6)} %select_n.4), kind=kLoop, calls=%fused_computation | loop fusion | flops 524288 | bytes 4194308 | tf_op jit(solution)/shard_map/div | solution.py:158
Async XLA Ops:
  7.2 176.3 %all-reduce.2.cloned.1.call-start = ((), (), s32[]{:S(2)}) async-start(), calls=%async_computation.1 | async-start | bytes 8388608 | tf_op jit(solution)/shard_map/psum | solution.py:152
  15.9 5.1 %copy-start = (f32[2,32,8,512]{3,2,0,1:T(8,128)}, f32[2,32,8,512]{3,2,0,1:T(8,128)S(1)}, u32[]{:S(2)}) copy-start(f32[2,32,8,512]{3,2,0,1:T(8,128)S(1)} %copy.4) | copy-start | bytes 3145732
Sparse Core Ops, SparseCore 0:
  21.1 162.2 all-reduce.1

commit v2 on v1

--- a/solution.py
+++ b/solution.py
@@ -1,3 +1,5 @@
+import functools
+
 import jax
 import jax.numpy as jnp
 from jax import lax
@@ -86,9 +88,9 @@
 
 
 def factor_kernel(gram_ref, rows_ref, solved_ref, upper_ref, work, lhs, rhs):
-    n = gram_ref.shape[0]
-    full = n + rows_ref.shape[0]
-    work[:n] = gram_ref[...]
+    full, n = work.shape
+    for at, (i, j) in enumerate(lower_blocks(n // BLOCK)):
+        work[i * BLOCK : (i + 1) * BLOCK, j * BLOCK : (j + 1) * BLOCK] = gram_ref[at]
     work[n:] = rows_ref[...]
     for c0 in range(0, n, BLOCK):
         c1 = c0 + BLOCK
@@ -117,7 +119,7 @@
 
 
 def factor_and_solve(gram, rows):
-    n, m = gram.shape[0], rows.shape[0]
+    m, n = rows.shape
     return pl.pallas_call(
         factor_kernel,
         out_shape=[jax.ShapeDtypeStruct((m, n), f32), jax.ShapeDtypeStruct((n, n), f32)],
@@ -130,27 +132,239 @@
     )(gram, rows)
 
 
-def in_order(parts, dim):
-    dims = list(parts.shape[1:])
-    dims[dim] *= parts.shape[0]
-    return jnp.moveaxis(parts, 0, dim).reshape(dims)
-
-
-def from_everyone(value, axis):
-    size = lax.axis_size(axis)
-    return lax.all_to_all(
-        jnp.broadcast_to(value[None], (size, *value.shape)), axis, 0, 0, tiled=True
+CHUNK_BLOCKS = (4, 4, 4, 4, 2)
+
+
+def lower_blocks(count):
+    return [(i, j) for j in range(count) for i in range(j, count)]
+
+
+def remote(src, dst, send, recv, place):
+    return pltpu.make_async_remote_copy(
+        src_ref=src,
+        dst_ref=dst,
+        send_sem=send,
+        recv_sem=recv,
+        device_id=place,
+        device_id_type=pl.DeviceIdType.MESH,
     )
 
 
+def gram_kernel(nx, nz, mine_ref, gram_ref, whole_ref, lhs, rhs, part, in_f, in_s, in_z,
+                swap_sems, pair_sems, z_send, z_recv, g_send, g_recv):
+    rows_id = lax.axis_index("rows")
+    core = lax.axis_index("tensor")
+    x, z = rows_id // nz, rows_id % nz
+    near = x + 1 - 2 * (x % 2)
+    far = nx - 1 - x
+    high = x // 2
+    low = (high + x % 2) % 2
+    first = (1 - core) * near + core * far
+    second = (1 - core) * far + core * near
+    bit_f = (1 - core) * low + core * high
+    bit_s = (1 - core) * high + core * low
+    to_core = {"rows": rows_id, "tensor": 1 - core}
+    to_first = {"rows": first * nz + z, "tensor": core}
+    to_second = {"rows": second * nz + z, "tensor": core}
+
+    def to_z(step):
+        return {"rows": x * nz + (z + step) % nz, "tensor": core}
+
+    barrier = pltpu.get_barrier_semaphore()
+    places = [to_core, to_first, to_second] + [to_z(s) for s in range(1, nz)]
+    for place in places:
+        pl.semaphore_signal(
+            barrier, inc=1, device_id=place, device_id_type=pl.DeviceIdType.MESH
+        )
+    pl.semaphore_wait(barrier, len(places))
+
+    m, width = mine_ref.shape
+    own = pl.ds(pl.multiple_of(core * width, width), width)
+    swap = remote(mine_ref, whole_ref.at[:, own], swap_sems.at[0], swap_sems.at[1], to_core)
+    swap.start()
+    whole_ref[:, own] = mine_ref[...]
+    swap.wait()
+    for c in range(0, 2 * width, BLOCK):
+        parts = split3(whole_ref[:, c : c + BLOCK].T)
+        lhs[c : c + BLOCK] = left(parts, 1)
+        rhs[c : c + BLOCK] = right(parts, 1)
+
+    blocks = lower_blocks(2 * width // BLOCK)
+    starts = [sum(CHUNK_BLOCKS[:i]) for i in range(len(CHUNK_BLOCKS) + 1)]
+
+    def base_of(i):
+        return 2 * starts[i] + core * CHUNK_BLOCKS[i]
+
+    def quarter(i, ref, at, which):
+        n = CHUNK_BLOCKS[i]
+        if n == 4:
+            return ref.at[at + which]
+        half = BLOCK // 2
+        return ref.at[at + which // 2, pl.ds(pl.multiple_of((which % 2) * half, half), half)]
+
+    def half(i, ref, at, which):
+        n = CHUNK_BLOCKS[i] // 2
+        return ref.at[pl.ds(at + n * which, n)]
+
+    def piece(i, view, index):
+        n = CHUNK_BLOCKS[i] * BLOCK // (nx * nz)
+        return view.at[pl.ds(pl.multiple_of(index * n, n), n)]
+
+    def copy_first(i):
+        return remote(
+            half(i, part, starts[i], 1 - bit_f), half(i, in_f, starts[i] // 2, 0),
+            pair_sems.at[i, 0], pair_sems.at[i, 1], to_first)
+
+    def arrived(i, ref, which):
+        return ref.at[i] if CHUNK_BLOCKS[i] == 4 else ref.at[i, pl.ds(0, BLOCK // 2)]
+
+    def copy_second(i):
+        return remote(
+            quarter(i, part, starts[i], 2 * bit_f + 1 - bit_s), arrived(i, in_s, 0),
+            pair_sems.at[i, 2], pair_sems.at[i, 3], to_second)
+
+    def own_part(i):
+        return quarter(i, part, starts[i], 2 * bit_f + bit_s)
+
+    def own_gram(i):
+        return quarter(i, gram_ref, base_of(i), 2 * bit_f + bit_s)
+
+    def in_piece(i, index):
+        n = CHUNK_BLOCKS[i] * BLOCK // (nx * nz)
+        return in_z.at[i, index, pl.ds(0, n)]
+
+    def copy_z(i, step):
+        return remote(
+            piece(i, own_part(i), (z + step) % nz), in_piece(i, nz - step),
+            z_send.at[i, step], z_recv.at[i, nz - step], to_z(step))
+
+    def copy_z_in(i, step):
+        return remote(
+            piece(i, own_part(i), z), in_piece(i, step),
+            z_send.at[i, step], z_recv.at[i, step], to_z(step))
+
+    def copy_gather(i, step):
+        mine = piece(i, own_gram(i), z)
+        return remote(mine, mine, g_send.at[i, step], g_recv.at[i, nz - step], to_z(step))
+
+    def copy_gather_in(i, step):
+        theirs = piece(i, own_gram(i), (z + step) % nz)
+        return remote(theirs, theirs, g_send.at[i, step], g_recv.at[i, step], to_z(step))
+
+    def copy_back_second(i, bit):
+        view = quarter(i, gram_ref, base_of(i), 2 * bit_f + bit)
+        return remote(view, view, pair_sems.at[i, 4], pair_sems.at[i, 5], to_second)
+
+    def copy_back_first(i, bit):
+        view = half(i, gram_ref, base_of(i), bit)
+        return remote(view, view, pair_sems.at[i, 6], pair_sems.at[i, 7], to_first)
+
+    def copy_core(i, side):
+        view = gram_ref.at[pl.ds(2 * starts[i] + side * CHUNK_BLOCKS[i], CHUNK_BLOCKS[i])]
+        return remote(view, view, pair_sems.at[i, 8], pair_sems.at[i, 9], to_core)
+
+    def stage_gram(i):
+        for q in range(CHUNK_BLOCKS[i]):
+            a, b = blocks[2 * starts[i] + q], blocks[2 * starts[i] + CHUNK_BLOCKS[i] + q]
+            bi = pl.multiple_of((a[0] + core * (b[0] - a[0])) * BLOCK, BLOCK)
+            bj = pl.multiple_of((a[1] + core * (b[1] - a[1])) * BLOCK, BLOCK)
+            part[starts[i] + q] = dot_over(lhs[pl.ds(bi, BLOCK)], rhs[pl.ds(bj, BLOCK)], 1)
+        copy_first(i).start()
+
+    def stage_first(i):
+        copy_first(i).wait()
+        n = CHUNK_BLOCKS[i] // 2
+        at = pl.ds(starts[i] + n * bit_f, n)
+        part[at] += in_f[pl.ds(starts[i] // 2, n)]
+        copy_second(i).start()
+
+    def stage_second(i):
+        copy_second(i).wait()
+        mine = own_part(i)
+        mine[...] += arrived(i, in_s, 0)[...]
+        for step in range(1, nz):
+            copy_z(i, step).start()
+
+    def stage_scatter(i):
+        total = piece(i, own_part(i), z)[...]
+        for step in range(1, nz):
+            copy_z_in(i, step).wait_recv()
+            total = total + in_piece(i, step)[...]
+        piece(i, own_gram(i), z)[...] = total
+        for step in range(1, nz):
+            copy_gather(i, step).start()
+
+    def stage_gather(i):
+        for step in range(1, nz):
+            copy_gather_in(i, step).wait_recv()
+        copy_back_second(i, bit_s).start()
+
+    def stage_back_second(i):
+        copy_back_second(i, 1 - bit_s).wait_recv()
+        copy_back_first(i, bit_f).start()
+
+    def stage_back_first(i):
+        copy_back_first(i, 1 - bit_f).wait_recv()
+        copy_core(i, core).start()
+
+    def stage_core(i):
+        copy_core(i, 1 - core).wait_recv()
+
+    stages = (stage_gram, stage_first, stage_second, stage_scatter, stage_gather,
+              stage_back_second, stage_back_first, stage_core)
+    chunks = len(CHUNK_BLOCKS)
+    for t in range(chunks + len(stages) - 1):
+        for s in reversed(range(len(stages))):
+            if 0 <= t - s < chunks:
+                stages[s](t - s)
+    for i in range(chunks):
+        for step in range(1, nz):
+            copy_z(i, step).wait_send()
+            copy_gather(i, step).wait_send()
+        copy_back_second(i, bit_s).wait_send()
+        copy_back_first(i, bit_f).wait_send()
+        copy_core(i, core).wait_send()
+
+
+def reduced_gram(mine, nx, nz):
+    m, width = mine.shape
+    n = 2 * width
+    count = len(lower_blocks(n // BLOCK))
+    chunks = len(CHUNK_BLOCKS)
+    dma = pltpu.SemaphoreType.DMA
+    return pl.pallas_call(
+        functools.partial(gram_kernel, nx, nz),
+        out_shape=[
+            jax.ShapeDtypeStruct((count, BLOCK, BLOCK), f32),
+            jax.ShapeDtypeStruct((m, n), f32),
+        ],
+        in_specs=[pl.BlockSpec(memory_space=pltpu.VMEM)],
+        out_specs=[pl.BlockSpec(memory_space=pltpu.VMEM)] * 2,
+        scratch_shapes=[
+            pltpu.VMEM((n, 6 * m), bf16),
+            pltpu.VMEM((n, 6 * m), bf16),
+            pltpu.VMEM((count // 2, BLOCK, BLOCK), f32),
+            pltpu.VMEM((count // 4, BLOCK, BLOCK), f32),
+            pltpu.VMEM((chunks, BLOCK, BLOCK), f32),
+            pltpu.VMEM((chunks, nz, 16, BLOCK), f32),
+            dma((2,)),
+            dma((chunks, 10)),
+            dma((chunks, nz)),
+            dma((chunks, nz)),
+            dma((chunks, nz)),
+            dma((chunks, nz)),
+        ],
+        compiler_params=pltpu.CompilerParams(
+            collective_id=0, has_side_effects=True, vmem_limit_bytes=60 * 2**20
+        ),
+    )(mine)
+
+
 def shards(effects):
-    whole = in_order(from_everyone(effects, "tensor"), 1)
+    nx, nz = 4, lax.axis_size("rows") // 4
+    gram, whole = reduced_gram(effects, nx, nz)
+    solved, upper = factor_and_solve(gram, whole)
     width = effects.shape[1]
-    local_gram = jnp.dot(
-        whole.T, whole, precision=lax.Precision.HIGHEST, preferred_element_type=jnp.float32
-    )
-    gram = lax.psum(local_gram, "rows")
-    solved, upper = factor_and_solve(gram, whole)
     total = effects.shape[0] * lax.axis_size("rows")
     scale = jnp.sqrt(jnp.float32(total))
     start = lax.axis_index("tensor") * width

time: 233 us -> 106 us (0.45)
  waiting for transfers between devices: 162 us -> 0 us
  Pallas kernels: 34.9 us -> 99.5 us
  between operations: 14.1 us -> 0.64 us
  blocking collectives: 7.4 us -> 0 us
  matrix products: 5.06 us -> 0 us
    psum x1 -> x0, waiting for transfers between devices: 162 us -> none  [shards(): gram = lax.psum(local_gram, 'rows')]
    pallas_call x0 -> x1, Pallas kernels: none -> 64.9 us  [reduced_gram(): pl.pallas_call(functools.partial(gram_kernel, nx, nz), out_shape=[jax.Sha...]
    all_to_all x1 -> x0, blocking collectives: 7.4 us -> none  [from_everyone(): lax.all_to_all(jnp.broadcast_to(value[None], (size, *value.shape)), axis,...]
    dot_general x1 -> x0, matrix products: 5.06 us -> none  [shards(): jnp.dot(whole.T, whole, precision=lax.Precision.HIGHEST, preferred_elemen...]
  transfers between devices with their start and end apart: 1 -> 0, of which waited for: 1 -> 0; matrix products, arithmetic and copies ran while one was open for 0% -> 0% of each run, Pallas kernels for 0% -> 0%
where the time goes in v2:
time: 106 us; the launch traced here: 105 us
  Pallas kernels  99.5 us (94%)
  other arithmetic  5.04 us (5%)
    pallas_call x1, Pallas kernels, reduced_gram(): pl.pallas_call(functools.partial(gram_kernel, nx, nz), out_shape=[jax.Sha...  64.9 us
    pallas_call x1, Pallas kernels, factor_and_solve(): pl.pallas_call(factor_kernel, out_shape=[jax.ShapeDtypeStruct((m, n), f32...  34.6 us
    div x1, other arithmetic, shards(): triangle = lax.dynamic_slice_in_dim(upper, start, width, 1) / scale  3.15 us

profile of v2, /device:TPU:1, one launch (start us, length us, event | category | flops | bytes accessed | tf_op | source)
XLA Modules:
  0.0 105.1 jit_solution(5810328674143873671)
XLA Ops:
  0.6 64.9 %shard_map.30 = (f32[36,128,128]{2,1,0:T(8,128)}, f32[256,1024]{1,0:T(8,128)}) custom-call(f32[256,512]{1,0:T(8,128)} %mine_ref.1), custom_call_target="tpu_custom_call" | custom-call | tf_op jit(solution)/shard_map/pallas_call | solution.py:335
  65.5 34.6 %shard_map.31 = (f32[256,1024]{1,0:T(8,128)}, f32[1024,1024]{1,0:T(8,128)}) custom-call(f32[36,128,128]{2,1,0:T(8,128)} %get-tuple-element.6.gram_ref, f32[256,1024]{1,0:T(8,128)} %get-tuple-element.7.rows_ref), custom_call_target="tpu_custom_call" | custom-call | tf_op jit(solution)/shard_map/pallas_call | solution.py:123
  100.1 1.9 %dynamic-slice_multiply_fusion.1 = f32[256,512]{1,0:T(8,128)} fusion(f32[256,1024]{1,0:T(8,128)} %get-tuple-element.8, s32[]{:T(128)S(6)} %select_n.4), kind=kLoop, calls=%fused_computation.1 | loop fusion | flops 131072 | bytes 1048580 | tf_op jit(solution)/shard_map/mul | solution.py:371
  102.0 3.2 %dynamic-slice_multiply_fusion = f32[1024,512]{1,0:T(8,128)} fusion(f32[1024,1024]{1,0:T(8,128)} %get-tuple-element.9, s32[]{:T(128)S(6)} %select_n.4), kind=kLoop, calls=%fused_computation | loop fusion | flops 524288 | bytes 4194308 | tf_op jit(solution)/shard_map/div | solution.py:372

commit v3 on v2

v3 whole, which is shorter than its diff:
```python
import functools

import jax
import jax.numpy as jnp
from jax import lax
from jax.experimental import pallas as pl
from jax.experimental.pallas import tpu as pltpu
from jax.sharding import PartitionSpec as P

f32 = jnp.float32
bf16 = jnp.bfloat16
BLOCK = 128
BASE = 32


def split3(x):
    high = x.astype(bf16)
    rest = x - high.astype(f32)
    middle = rest.astype(bf16)
    return high, middle, (rest - middle.astype(f32)).astype(bf16)


def left(parts, dim):
    h, m, l = parts
    return jnp.concatenate([h, h, m, h, m, l], dim)


def right(parts, dim):
    h, m, l = parts
    return jnp.concatenate([h, m, h, l, m, h], dim)


def dot_over(a, b, dim):
    return lax.dot_general(a, b, (((dim,), (dim,)), ((), ())), preferred_element_type=f32)


def eliminate(rows, offset):
    tiles = BASE // 8
    cols = [
        [
            jnp.broadcast_to(rows[8 * t : 8 * t + 8, offset + j : offset + j + 1], (8, BLOCK))
            for t in range(tiles)
        ]
        for j in range(BASE)
    ]
    panel = [
        [rows[8 * t : 8 * t + 8, BLOCK * c : BLOCK * (c + 1)] for c in range(2)]
        for t in range(tiles)
    ]
    row = lax.broadcasted_iota(jnp.int32, (8, BLOCK), 0)
    scales = [jnp.zeros((8, BLOCK), f32) for _ in range(tiles)]
    for j in range(BASE):
        t0, r = divmod(j, 8)
        inv = lax.rsqrt(jnp.broadcast_to(cols[j][t0][r : r + 1], (8, BLOCK)))
        scales[t0] = jnp.where(row == r, inv, scales[t0])
        column = [cols[j][t] * inv for t in range(t0, tiles)]
        below = [jnp.where(row > r, column[0], 0.0)] + column[1:]
        pivot = [jnp.broadcast_to(panel[t0][c][r : r + 1], (8, BLOCK)) * inv for c in range(2)]
        for t in range(t0, tiles):
            for c in range(2):
                panel[t][c] = panel[t][c] - below[t - t0] * pivot[c]
        for j2 in range(j + 1, BASE):
            t2, r2 = divmod(j2, 8)
            factor = jnp.broadcast_to(column[t2 - t0][r2 : r2 + 1], (8, BLOCK))
            for t in range(t2, tiles):
                cols[j2][t] = cols[j2][t] - column[t - t0] * factor
    return jnp.concatenate(
        [jnp.concatenate([panel[t][c] * scales[t] for c in range(2)], 1) for t in range(tiles)], 0
    )


def factor_block(block):
    shape = (BLOCK, BLOCK)
    row = lax.broadcasted_iota(jnp.int32, shape, 0)
    col = lax.broadcasted_iota(jnp.int32, shape, 1)
    rest = jnp.concatenate([block, jnp.where(row == col, 1.0, 0.0).astype(f32)], 1)
    done = []
    for s in range(0, BLOCK, BASE):
        rows = eliminate(rest[:BASE], s)
        at = lax.broadcasted_iota(jnp.int32, rows.shape, 1)
        diag = lax.broadcasted_iota(jnp.int32, rows.shape, 0) + s
        rows = jnp.where(at < jnp.minimum(diag, BLOCK), 0.0, rows)
        done.append(rows)
        if s + BASE < BLOCK:
            update = dot_over(left(split3(rows[:, :BLOCK]), 0), right(split3(rows), 0), 0)
            rest = rest[BASE:] - update[s + BASE :]
        yield
    return jnp.concatenate(done, 0)


def factor_steps(work, lhs, rhs, n, base, first, last, put_upper, put_solved):
    full = work.shape[0] + base
    for c0 in range(first, last, BLOCK):
        yield c0
        c1 = c0 + BLOCK
        cols = slice(c0 - base, c1 - base)
        factored = yield from factor_block(work[cols, cols])
        put_upper(c0, c0, factored[:, :BLOCK])
        inverse = right(split3(factored[:, BLOCK:]), 1)
        for r in range(c1, full, BLOCK):
            at = slice(r - base, r - base + BLOCK)
            solved = dot_over(left(split3(work[at, cols]), 1), inverse, 1)
            parts = split3(solved)
            lhs[at] = left(parts, 1)
            if r >= n:
                put_solved(r - n, c0, solved)
            else:
                put_upper(c0, r, solved.T)
                rhs[at] = right(parts, 1)
        yield
        j = c1
        while j < n:
            width = BLOCK if (j // BLOCK) % 2 else min(2 * BLOCK, n - j)
            to = slice(j - base, j - base + width)
            against = rhs[to]
            spans = [(r, min(2 * BLOCK, n - r)) for r in range(j, n, 2 * BLOCK)]
            spans += [(r, min(2 * BLOCK, full - r)) for r in range(n, full, 2 * BLOCK)]
            for r, h in spans:
                at = slice(r - base, r - base + h)
                product = dot_over(lhs[at], against, 1)
                if c0 == 0 and r < n:
                    work[at, to] = -product
                else:
                    work[at, to] -= product
            j += width
            yield


CHUNK_BLOCKS = (4, 4, 4, 4, 2)
CHUNK_STARTS = (0, 2.5, 5, 7.5, 10)
STAGE_TIMES = (
    ("S", 2.9, 0.37),
    ("Z", 2.0, 0.18),
    ("A", 2.8, 0.4),
    ("B", 4.6, 0.4),
    ("C", 3.1, 0.18),
    ("D", 2.6, 0.37),
    ("E", 1.2, 0.1),
    ("W", 0.1, 0.0),
)
FRONT_STEPS = 6
PACE = 1


def stage_order():
    timed = [(0.0, 1, "P", c) for c in range(4)]
    for i, (start, n) in enumerate(zip(CHUNK_STARTS, CHUNK_BLOCKS)):
        timed.append((start - 1.0, 2 if i else 0, "G", i))
        timed.append((start - 1.0 if i == 0 else start, 3 if i else 0, "F", i))
        at = start
        for name, fixed, each in STAGE_TIMES:
            at += fixed + each * n
            timed.append((at, 4 + i, name, i))
    first = [("P", 0)]
    return first + [e[2:] for e in sorted(timed, key=lambda e: e[:2]) if e[2:] != first[0]]


def lower_blocks(count):
    return [(i, j) for j in range(count) for i in range(j, count)]


def remote(src, dst, send, recv, place):
    return pltpu.make_async_remote_copy(
        src_ref=src,
        dst_ref=dst,
        send_sem=send,
        recv_sem=recv,
        device_id=place,
        device_id_type=pl.DeviceIdType.MESH,
    )


def front_kernel(nx, nz, mine_ref, rest_ref, top_ref, first_ref, work, upper, solved, gram_ref,
                 lhs, rhs,
                 panel_l, panel_r, part, in_f, in_s, in_z,
                 fetch_sem, swap_send, swap_recv, pair_sems, z_send, z_recv, g_send, g_recv):
    m, width = mine_ref.shape
    n = 2 * width
    whole_ref = work.at[pl.ds(n, m)]
    rows_id = lax.axis_index("rows")
    core = lax.axis_index("tensor")
    x, z = rows_id // nz, rows_id % nz
    near = x + 1 - 2 * (x % 2)
    far = nx - 1 - x
    high = x // 2
    low = (high + x % 2) % 2
    first = (1 - core) * near + core * far
    second = (1 - core) * far + core * near
    bit_f = (1 - core) * low + core * high
    bit_s = (1 - core) * high + core * low
    to_core = {"rows": rows_id, "tensor": 1 - core}
    to_first = {"rows": first * nz + z, "tensor": core}
    to_second = {"rows": second * nz + z, "tensor": core}

    def to_z(step):
        return {"rows": x * nz + (z + step) % nz, "tensor": core}

    own = pl.ds(pl.multiple_of(core * width, width), width)
    barrier = pltpu.get_barrier_semaphore()
    places = [to_core, to_first, to_second] + [to_z(s) for s in range(1, nz)]
    for place in places:
        pl.semaphore_signal(
            barrier, inc=1, device_id=place, device_id_type=pl.DeviceIdType.MESH
        )
    pieces = width // BLOCK
    fetch = pltpu.make_async_copy(mine_ref, whole_ref.at[:, own], fetch_sem)
    fetch.start()
    upper[...] = jnp.zeros(upper.shape, f32)
    fetch.wait()

    def columns(side, piece):
        return pl.ds(pl.multiple_of(side * width + piece * BLOCK, BLOCK), BLOCK)

    def prepare(side, piece):
        at = columns(side, piece)
        parts = split3(whole_ref[:, at].T)
        lhs[at] = left(parts, 1)
        rhs[at] = right(parts, 1)

    def swap(side, piece):
        view = whole_ref.at[:, columns(side, piece)]
        return remote(view, view, swap_send.at[piece], swap_recv.at[piece], to_core)

    for c in range(pieces):
        prepare(core, c)
    pl.semaphore_wait(barrier, len(places))
    for c in range(pieces):
        swap(core, c).start()

    def stage_swap(c):
        swap(core, c).wait_send()
        swap(1 - core, c).wait_recv()
        prepare(1 - core, c)

    blocks = lower_blocks(2 * width // BLOCK)
    starts = [sum(CHUNK_BLOCKS[:i]) for i in range(len(CHUNK_BLOCKS) + 1)]

    def span(ref, start, rows):
        return ref.at[pl.ds(pl.multiple_of(start, 8), rows)]

    def half(i, ref, at, which):
        rows = CHUNK_BLOCKS[i] * BLOCK // 2
        return span(ref, at + rows * which, rows)

    def quarter(i, ref, at, which):
        rows = CHUNK_BLOCKS[i] * BLOCK // 4
        return span(ref, at + rows * which, rows)

    def piece(i, ref, at, index):
        rows = CHUNK_BLOCKS[i] * BLOCK // (nx * nz)
        return span(ref, at + rows * index, rows)

    def part_of(i):
        return starts[i] * BLOCK

    def gram_of(i, side):
        return (2 * starts[i] + side * CHUNK_BLOCKS[i]) * BLOCK

    def copy_first(i):
        return remote(
            half(i, part, part_of(i), 1 - bit_f), half(i, in_f, part_of(i) // 2, 0),
            pair_sems.at[i, 0], pair_sems.at[i, 1], to_first)

    def copy_second(i):
        return remote(
            quarter(i, part, part_of(i), 2 * bit_f + 1 - bit_s),
            quarter(i, in_s, part_of(i) // 4, 0),
            pair_sems.at[i, 2], pair_sems.at[i, 3], to_second)

    def own_part(i):
        return part_of(i) + (2 * bit_f + bit_s) * (CHUNK_BLOCKS[i] * BLOCK // 4)

    def own_gram(i):
        return gram_of(i, core) + (2 * bit_f + bit_s) * (CHUNK_BLOCKS[i] * BLOCK // 4)

    def in_piece(i, index):
        return piece(i, in_z, part_of(i) // nx, index)

    def copy_z(i, step):
        return remote(
            piece(i, part, own_part(i), (z + step) % nz), in_piece(i, nz - step),
            z_send.at[i, step], z_recv.at[i, nz - step], to_z(step))

    def copy_z_in(i, step):
        return remote(
            piece(i, part, own_part(i), z), in_piece(i, step),
            z_send.at[i, step], z_recv.at[i, step], to_z(step))

    def copy_gather(i, step):
        mine = piece(i, gram_ref, own_gram(i), z)
        return remote(mine, mine, g_send.at[i, step], g_recv.at[i, nz - step], to_z(step))

    def copy_gather_in(i, step):
        theirs = piece(i, gram_ref, own_gram(i), (z + step) % nz)
        return remote(theirs, theirs, g_send.at[i, step], g_recv.at[i, step], to_z(step))

    def copy_back_second(i, bit):
        view = quarter(i, gram_ref, gram_of(i, core), 2 * bit_f + bit)
        return remote(view, view, pair_sems.at[i, 4], pair_sems.at[i, 5], to_second)

    def copy_back_first(i, bit):
        view = half(i, gram_ref, gram_of(i, core), bit)
        return remote(view, view, pair_sems.at[i, 6], pair_sems.at[i, 7], to_first)

    def copy_core(i, side):
        view = span(gram_ref, gram_of(i, side), CHUNK_BLOCKS[i] * BLOCK)
        return remote(view, view, pair_sems.at[i, 8], pair_sems.at[i, 9], to_core)

    def stage_gram(i):
        for q in range(CHUNK_BLOCKS[i]):
            a, b = blocks[2 * starts[i] + q], blocks[2 * starts[i] + CHUNK_BLOCKS[i] + q]
            bi = pl.multiple_of((a[0] + core * (b[0] - a[0])) * BLOCK, BLOCK)
            bj = pl.multiple_of((a[1] + core * (b[1] - a[1])) * BLOCK, BLOCK)
            at = (starts[i] + q) * BLOCK
            part[at : at + BLOCK] = dot_over(lhs[pl.ds(bi, BLOCK)], rhs[pl.ds(bj, BLOCK)], 1)

    def stage_send(i):
        copy_first(i).start()

    def stage_first(i):
        copy_first(i).wait()
        half(i, part, part_of(i), bit_f)[...] += half(i, in_f, part_of(i) // 2, 0)[...]
        copy_second(i).start()

    def stage_second(i):
        copy_second(i).wait()
        mine = quarter(i, part, own_part(i), 0)
        mine[...] += quarter(i, in_s, part_of(i) // 4, 0)[...]
        for step in range(1, nz):
            copy_z(i, step).start()

    def stage_scatter(i):
        total = piece(i, part, own_part(i), z)[...]
        for step in range(1, nz):
            copy_z_in(i, step).wait_recv()
            total = total + in_piece(i, step)[...]
        piece(i, gram_ref, own_gram(i), z)[...] = total
        for step in range(1, nz):
            copy_gather(i, step).start()

    def stage_gather(i):
        for step in range(1, nz):
            copy_gather_in(i, step).wait_recv()
        copy_back_second(i, bit_s).start()

    def stage_back_second(i):
        copy_back_second(i, 1 - bit_s).wait_recv()
        copy_back_first(i, bit_f).start()

    def stage_back_first(i):
        copy_back_first(i, 1 - bit_f).wait_recv()
        copy_core(i, core).start()

    def stage_core(i):
        copy_core(i, 1 - core).wait_recv()

    def stage_add(i):
        for at in range(2 * starts[i], 2 * starts[i + 1]):
            bi, bj = blocks[at]
            to = slice(bi * BLOCK, (bi + 1) * BLOCK), slice(bj * BLOCK, (bj + 1) * BLOCK)
            block = gram_ref[at * BLOCK : (at + 1) * BLOCK]
            if bj == 0:
                work[to] = block
            else:
                work[to] += block

    stages = dict(
        P=stage_swap, G=stage_gram, F=stage_send, S=stage_first, Z=stage_second, A=stage_scatter,
        B=stage_gather, C=stage_back_second, D=stage_back_first, E=stage_core, W=stage_add)
    todo = stage_order()

    def run(count, updated):
        while todo and count:
            name, i = todo[0]
            if name == "W" and i > 0 and not updated:
                return
            todo.pop(0)
            stages[name](i)
            count -= 1

    def put_upper(row, col, block):
        upper[row : row + BLOCK, col : col + BLOCK] = block

    def put_solved(row, col, block):
        solved[row : row + BLOCK, col : col + BLOCK] = block

    chunks = len(CHUNK_BLOCKS)
    middle = upper.shape[0]
    for at in factor_steps(work, panel_l, panel_r, n, 0, 0, middle, put_upper, put_solved):
        if at is not None:
            c0 = at
            need = max(i for i in range(chunks) if blocks[2 * starts[i]][1] * BLOCK <= c0)
            while ("W", need) in todo:
                run(1, c0 > 0)
        else:
            run(PACE, c0 > 0)
    run(len(todo), True)
    scale = jnp.sqrt(jnp.float32(m * nx * nz))
    top_ref[...] = upper[:, own] / scale
    first_ref[...] = solved[:, own] * scale
    rest_ref[...] = work[middle:, middle:]
    for i in range(chunks):
        for step in range(1, nz):
            copy_z(i, step).wait_send()
            copy_gather(i, step).wait_send()
        copy_back_second(i, bit_s).wait_send()
        copy_back_first(i, bit_f).wait_send()
        copy_core(i, core).wait_send()


def front(mine, nx, nz):
    m, width = mine.shape
    n = 2 * width
    middle = FRONT_STEPS * BLOCK
    count = len(lower_blocks(n // BLOCK))
    chunks = len(CHUNK_BLOCKS)
    dma = pltpu.SemaphoreType.DMA
    return pl.pallas_call(
        functools.partial(front_kernel, nx, nz),
        out_shape=[
            jax.ShapeDtypeStruct((n + m - middle, n - middle), f32),
            jax.ShapeDtypeStruct((middle, width), f32),
            jax.ShapeDtypeStruct((m, width), f32),
        ],
        in_specs=[pl.BlockSpec(memory_space=pltpu.HBM)],
        out_specs=[pl.BlockSpec(memory_space=pltpu.VMEM)] * 3,
        scratch_shapes=[
            pltpu.VMEM((n + m, n), f32),
            pltpu.VMEM((middle, n), f32),
            pltpu.VMEM((m, n), f32),
            pltpu.VMEM((count * BLOCK, BLOCK), f32),
            pltpu.VMEM((n, 6 * m), bf16),
            pltpu.VMEM((n, 6 * m), bf16),
            pltpu.VMEM((n + m, 6 * BLOCK), bf16),
            pltpu.VMEM((n, 6 * BLOCK), bf16),
            pltpu.VMEM((count * BLOCK // 2, BLOCK), f32),
            pltpu.VMEM((count * BLOCK // 4, BLOCK), f32),
            pltpu.VMEM((count * BLOCK // 8, BLOCK), f32),
            pltpu.VMEM((count * BLOCK // (2 * nx), BLOCK), f32),
            dma(()),
            dma((4,)),
            dma((4,)),
            dma((chunks, 10)),
            dma((chunks, nz)),
            dma((chunks, nz)),
            dma((chunks, nz)),
            dma((chunks, nz)),
        ],
        compiler_params=pltpu.CompilerParams(
            collective_id=0, has_side_effects=True, vmem_limit_bytes=40 * 2**20
        ),
    )(mine)


def back_kernel(total, rest_ref, top_ref, first_ref, basis_ref, triangle_ref, work, lhs, rhs):
    core = lax.axis_index("tensor")
    base = top_ref.shape[0]
    n, width = triangle_ref.shape
    scale = jnp.sqrt(jnp.float32(total))
    work[...] = rest_ref[...]
    triangle_ref[:base] = top_ref[...]
    triangle_ref[base:] = jnp.zeros((n - base, width), f32)

    basis_ref[...] = first_ref[...]

    def put_upper(row, col, block):
        at = slice(row, row + BLOCK), slice(col - width, col - width + BLOCK)
        triangle_ref[at] = jnp.where(core == 1, block / scale, 0.0)

    def put_solved(row, col, block):
        at = slice(row, row + BLOCK), slice(col - width, col - width + BLOCK)
        basis_ref[at] = jnp.where(core == 1, block * scale, basis_ref[at])

    for _ in factor_steps(work, lhs, rhs, n, base, base, n, put_upper, put_solved):
        pass


def back(rest, top, first, total):
    m, width = first.shape
    n = 2 * width
    middle = top.shape[0]
    return pl.pallas_call(
        functools.partial(back_kernel, total),
        out_shape=[
            jax.ShapeDtypeStruct((m, width), f32),
            jax.ShapeDtypeStruct((n, width), f32),
        ],
        scratch_shapes=[
            pltpu.VMEM(rest.shape, f32),
            pltpu.VMEM((rest.shape[0], 6 * BLOCK), bf16),
            pltpu.VMEM((n - middle, 6 * BLOCK), bf16),
        ],
        compiler_params=pltpu.CompilerParams(vmem_limit_bytes=30 * 2**20),
    )(rest, top, first)


def shards(effects):
    nx, nz = 4, lax.axis_size("rows") // 4
    total = effects.shape[0] * lax.axis_size("rows")
    rest, top, first = front(effects, nx, nz)
    return tuple(back(rest, top, first, total))


def solution(mesh):
    in_specs = (P(("groups", "rows"), "tensor"),)
    out_specs = (P(("groups", "rows"), "tensor"), P("groups", "tensor"))
    return jax.shard_map(shards, mesh=mesh, in_specs=in_specs, out_specs=out_specs, check_vma=False)
```

time: 106 us -> 78.8 us (0.74)
  Pallas kernels: 99.5 us -> 77 us
  other arithmetic: 5.04 us -> 0 us
    pallas_call x2, Pallas kernels: 99.5 us -> 77 us  [the longest x1 68.6 us: front(): pl.pallas_call(functools.partial(front_kernel, nx, nz), out_shape=[jax.Sh...]
    div x1 -> x0, other arithmetic: 3.15 us -> none  [shards(): triangle = lax.dynamic_slice_in_dim(upper, start, width, 1) / scale]
    mul x1 -> x0, other arithmetic: 1.88 us -> none  [shards(): basis = lax.dynamic_slice_in_dim(solved, start, width, 1) * scale]
where the time goes in v3:
time: 78.8 us; the launch traced here: 78.7 us
  Pallas kernels  77 us (98%)
  local copies, waits for them, and re-layouts  1.03 us (1%)
    pallas_call x1, Pallas kernels, front(): pl.pallas_call(functools.partial(front_kernel, nx, nz), out_shape=[jax.Sh...  68.6 us
    pallas_call x1, Pallas kernels, back(): pl.pallas_call(functools.partial(back_kernel, total), out_shape=[jax.Shap...  8.44 us

profile of v3, /device:TPU:1, one launch (start us, length us, event | category | flops | bytes accessed | tf_op | source)
XLA Modules:
  0.0 78.7 jit_solution(12002213575277501493)
XLA Ops:
  0.6 0.0 copy-start
  0.6 1.0 %copy-done = f32[256,512]{1,0:T(8,128)S(1)} copy-done((f32[256,512]{1,0:T(8,128)S(1)}, f32[256,512]{1,0:T(8,128)}, u32[]{:S(2)}) %copy-start) | copy-done | bytes 524312
  1.7 68.6 %shard_map.30 = (f32[512,256]{1,0:T(8,128)S(1)}, f32[768,512]{1,0:T(8,128)S(1)}, f32[256,512]{1,0:T(8,128)S(1)}) custom-call(f32[256,512]{1,0:T(8,128)S(1)} %copy-done), custom_call_target="tpu_custom_call" | custom-call | tf_op jit(solution)/shard_map/pallas_call | solution.py:418
  70.2 8.4 %shard_map.31 = (f32[256,512]{1,0:T(8,128)}, f32[1024,512]{1,0:T(8,128)}) custom-call(f32[512,256]{1,0:T(8,128)S(1)} %get-tuple-element.5.rest_ref, f32[768,512]{1,0:T(8,128)S(1)} %get-tuple-element.6.top_ref, f32[256,512]{1,0:T(8,128)S(1)} %get-tuple-element.7.first_ref), custom_call_target="tpu_custom_call" | custom-call | tf_op jit(solution)/shard_map/pallas_call | solution.py:482
Async XLA Ops:
  0.6 1.0 %copy-start = (f32[256,512]{1,0:T(8,128)S(1)}, f32[256,512]{1,0:T(8,128)}, u32[]{:S(2)}) copy-start(f32[256,512]{1,0:T(8,128)} %mine_ref.1) | copy-start | bytes 1572868

commit v4 on v3

--- a/solution.py
+++ b/solution.py
@@ -69,13 +69,17 @@
     )
 
 
-def factor_block(block):
+def factor_block(block, beside):
     shape = (BLOCK, BLOCK)
     row = lax.broadcasted_iota(jnp.int32, shape, 0)
     col = lax.broadcasted_iota(jnp.int32, shape, 1)
     rest = jnp.concatenate([block, jnp.where(row == col, 1.0, 0.0).astype(f32)], 1)
     done = []
-    for s in range(0, BLOCK, BASE):
+    parts = BLOCK // BASE
+    for p in range(parts):
+        s = p * BASE
+        for call in beside[len(beside) * p // parts : len(beside) * (p + 1) // parts]:
+            call()
         rows = eliminate(rest[:BASE], s)
         at = lax.broadcasted_iota(jnp.int32, rows.shape, 1)
         diag = lax.broadcasted_iota(jnp.int32, rows.shape, 0) + s
@@ -90,11 +94,17 @@
 
 def factor_steps(work, lhs, rhs, n, base, first, last, put_upper, put_solved):
     full = work.shape[0] + base
+
+    def update(r, h, j, w):
+        at = slice(r - base, r - base + h), slice(j - base, j - base + w)
+        work[at] -= dot_over(lhs[at[0]], rhs[at[1]], 1)
+
+    beside = []
     for c0 in range(first, last, BLOCK):
         yield c0
         c1 = c0 + BLOCK
         cols = slice(c0 - base, c1 - base)
-        factored = yield from factor_block(work[cols, cols])
+        factored = yield from factor_block(work[cols, cols], beside)
         put_upper(c0, c0, factored[:, :BLOCK])
         inverse = right(split3(factored[:, BLOCK:]), 1)
         for r in range(c1, full, BLOCK):
@@ -108,26 +118,26 @@
                 put_upper(c0, r, solved.T)
                 rhs[at] = right(parts, 1)
         yield
+        beside = []
         j = c1
         while j < n:
             width = BLOCK if (j // BLOCK) % 2 else min(2 * BLOCK, n - j)
-            to = slice(j - base, j - base + width)
-            against = rhs[to]
-            spans = [(r, min(2 * BLOCK, n - r)) for r in range(j, n, 2 * BLOCK)]
-            spans += [(r, min(2 * BLOCK, full - r)) for r in range(n, full, 2 * BLOCK)]
-            for r, h in spans:
-                at = slice(r - base, r - base + h)
-                product = dot_over(lhs[at], against, 1)
-                if c0 == 0 and r < n:
-                    work[at, to] = -product
-                else:
-                    work[at, to] -= product
+            top = j
+            if j == c1:
+                update(j, BLOCK, j, BLOCK)
+                if width > BLOCK:
+                    beside.append(functools.partial(update, j, BLOCK, j + BLOCK, BLOCK))
+                top = j + BLOCK
+            for r in range(top, full, 2 * BLOCK):
+                h = min(2 * BLOCK, full - r)
+                beside.append(functools.partial(update, r, h, j, width))
             j += width
-            yield
+    for call in beside:
+        call()
 
 
 CHUNK_BLOCKS = (4, 4, 4, 4, 2)
-CHUNK_STARTS = (0, 2.5, 5, 7.5, 10)
+CHUNK_STARTS = (0, 2, 4, 6, 8)
 STAGE_TIMES = (
     ("S", 2.9, 0.37),
     ("Z", 2.0, 0.18),
@@ -206,6 +216,7 @@
     fetch = pltpu.make_async_copy(mine_ref, whole_ref.at[:, own], fetch_sem)
     fetch.start()
     upper[...] = jnp.zeros(upper.shape, f32)
+    work[:n] = jnp.zeros((n, n), f32)
     fetch.wait()
 
     def columns(side, piece):
@@ -359,22 +370,16 @@
             bi, bj = blocks[at]
             to = slice(bi * BLOCK, (bi + 1) * BLOCK), slice(bj * BLOCK, (bj + 1) * BLOCK)
             block = gram_ref[at * BLOCK : (at + 1) * BLOCK]
-            if bj == 0:
-                work[to] = block
-            else:
-                work[to] += block
+            work[to] += block
 
     stages = dict(
         P=stage_swap, G=stage_gram, F=stage_send, S=stage_first, Z=stage_second, A=stage_scatter,
         B=stage_gather, C=stage_back_second, D=stage_back_first, E=stage_core, W=stage_add)
     todo = stage_order()
 
-    def run(count, updated):
+    def run(count):
         while todo and count:
-            name, i = todo[0]
-            if name == "W" and i > 0 and not updated:
-                return
-            todo.pop(0)
+            name, i = todo.pop(0)
             stages[name](i)
             count -= 1
 
@@ -391,10 +396,10 @@
             c0 = at
             need = max(i for i in range(chunks) if blocks[2 * starts[i]][1] * BLOCK <= c0)
             while ("W", need) in todo:
-                run(1, c0 > 0)
+                run(1)
         else:
-            run(PACE, c0 > 0)
-    run(len(todo), True)
+            run(PACE)
+    run(len(todo))
     scale = jnp.sqrt(jnp.float32(m * nx * nz))
     top_ref[...] = upper[:, own] / scale
     first_ref[...] = solved[:, own] * scale
@@ -452,20 +457,22 @@
     )(mine)
 
 
-def back_kernel(total, rest_ref, top_ref, first_ref, basis_ref, triangle_ref, work, lhs, rhs):
+def back_kernel(total, rest_ref, top_ref, first_ref, basis_ref, triangle_ref, work, lhs, rhs,
+                bottom, sems):
     core = lax.axis_index("tensor")
     base = top_ref.shape[0]
     n, width = triangle_ref.shape
     scale = jnp.sqrt(jnp.float32(total))
     work[...] = rest_ref[...]
-    triangle_ref[:base] = top_ref[...]
-    triangle_ref[base:] = jnp.zeros((n - base, width), f32)
+    put_top = pltpu.make_async_copy(top_ref, triangle_ref.at[pl.ds(0, base)], sems.at[0])
+    put_top.start()
+    bottom[...] = jnp.zeros(bottom.shape, f32)
 
     basis_ref[...] = first_ref[...]
 
     def put_upper(row, col, block):
-        at = slice(row, row + BLOCK), slice(col - width, col - width + BLOCK)
-        triangle_ref[at] = jnp.where(core == 1, block / scale, 0.0)
+        at = slice(row - base, row - base + BLOCK), slice(col - width, col - width + BLOCK)
+        bottom[at] = jnp.where(core == 1, block / scale, 0.0)
 
     def put_solved(row, col, block):
         at = slice(row, row + BLOCK), slice(col - width, col - width + BLOCK)
@@ -473,6 +480,12 @@
 
     for _ in factor_steps(work, lhs, rhs, n, base, base, n, put_upper, put_solved):
         pass
+    put_bottom = pltpu.make_async_copy(
+        bottom, triangle_ref.at[pl.ds(base, n - base)], sems.at[1]
+    )
+    put_bottom.start()
+    put_bottom.wait()
+    put_top.wait()
 
 
 def back(rest, top, first, total):
@@ -489,6 +502,12 @@
             pltpu.VMEM(rest.shape, f32),
             pltpu.VMEM((rest.shape[0], 6 * BLOCK), bf16),
             pltpu.VMEM((n - middle, 6 * BLOCK), bf16),
+            pltpu.VMEM((n - middle, width), f32),
+            pltpu.SemaphoreType.DMA((2,)),
+        ],
+        out_specs=[
+            pl.BlockSpec(memory_space=pltpu.VMEM),
+            pl.BlockSpec(memory_space=pltpu.HBM),
         ],
         compiler_params=pltpu.CompilerParams(vmem_limit_bytes=30 * 2**20),
     )(rest, top, first)

time: 78.8 us -> 81.2 us (1.030)
  Pallas kernels: 77 us -> 79.2 us
    pallas_call x1, Pallas kernels: 68.6 us -> 70.6 us  [front(): pl.pallas_call(functools.partial(front_kernel, nx, nz), out_shape=[jax.Sh...]
where the time goes in v4:
time: 81.2 us; the launch traced here: 81.1 us
  Pallas kernels  79.2 us (98%)
  local copies, waits for them, and re-layouts  1.03 us (1%)
  between operations  0.83 us (1%)
    pallas_call x1, Pallas kernels, front(): pl.pallas_call(functools.partial(front_kernel, nx, nz), out_shape=[jax.Sh...  70.6 us
    pallas_call x1, Pallas kernels, back(): pl.pallas_call(functools.partial(back_kernel, total), out_shape=[jax.Shap...  8.62 us

profile of v4, /device:TPU:1, one launch (start us, length us, event | category | flops | bytes accessed | tf_op | source)
XLA Modules:
  0.0 81.1 jit_solution(33989462194510460)
XLA Ops:
  0.6 0.0 copy-start
  0.6 1.0 %copy-done = f32[256,512]{1,0:T(8,128)S(1)} copy-done((f32[256,512]{1,0:T(8,128)S(1)}, f32[256,512]{1,0:T(8,128)}, u32[]{:S(2)}) %copy-start) | copy-done | bytes 524312
  1.7 70.6 %shard_map.30 = (f32[512,256]{1,0:T(8,128)S(1)}, f32[768,512]{1,0:T(8,128)S(1)}, f32[256,512]{1,0:T(8,128)S(1)}) custom-call(f32[256,512]{1,0:T(8,128)S(1)} %copy-done), custom_call_target="tpu_custom_call" | custom-call | tf_op jit(solution)/shard_map/pallas_call | solution.py:423
  72.3 8.6 %shard_map.31 = (f32[256,512]{1,0:T(8,128)}, f32[1024,512]{1,0:T(8,128)}) custom-call(f32[512,256]{1,0:T(8,128)S(1)} %get-tuple-element.5.rest_ref, f32[768,512]{1,0:T(8,128)S(1)} %get-tuple-element.6.top_ref, f32[256,512]{1,0:T(8,128)S(1)} %get-tuple-element.7.first_ref), custom_call_target="tpu_custom_call" | custom-call | tf_op jit(solution)/shard_map/pallas_call | solution.py:495
Async XLA Ops:
  0.6 1.0 %copy-start = (f32[256,512]{1,0:T(8,128)S(1)}, f32[256,512]{1,0:T(8,128)}, u32[]{:S(2)}) copy-start(f32[256,512]{1,0:T(8,128)} %mine_ref.1) | copy-start | bytes 1572868

commit v5 on v3

--- a/solution.py
+++ b/solution.py
@@ -126,8 +126,8 @@
             yield
 
 
-CHUNK_BLOCKS = (4, 4, 4, 4, 2)
-CHUNK_STARTS = (0, 2.5, 5, 7.5, 10)
+CHUNK_BLOCKS = (4, 4, 4, 6)
+CHUNK_STARTS = (0, 2.5, 5, 7.5)
 STAGE_TIMES = (
     ("S", 2.9, 0.37),
     ("Z", 2.0, 0.18),

time: 78.8 us -> 82 us (1.041)
  Pallas kernels: 77 us -> 80.2 us
    pallas_call x1, Pallas kernels: 68.6 us -> 71.8 us  [front(): pl.pallas_call(functools.partial(front_kernel, nx, nz), out_shape=[jax.Sh...]
where the time goes in v5:
time: 82 us; the launch traced here: 81.9 us
  Pallas kernels  80.2 us (98%)
  local copies, waits for them, and re-layouts  1.03 us (1%)
    pallas_call x1, Pallas kernels, front(): pl.pallas_call(functools.partial(front_kernel, nx, nz), out_shape=[jax.Sh...  71.8 us
    pallas_call x1, Pallas kernels, back(): pl.pallas_call(functools.partial(back_kernel, total), out_shape=[jax.Shap...  8.44 us

profile of v5, /device:TPU:1, one launch (start us, length us, event | category | flops | bytes accessed | tf_op | source)
XLA Modules:
  0.0 81.9 jit_solution(10107446915815992928)
XLA Ops:
  0.6 0.0 copy-start
  0.6 1.0 %copy-done = f32[256,512]{1,0:T(8,128)S(1)} copy-done((f32[256,512]{1,0:T(8,128)S(1)}, f32[256,512]{1,0:T(8,128)}, u32[]{:S(2)}) %copy-start) | copy-done | bytes 524312
  1.7 71.8 %shard_map.30 = (f32[512,256]{1,0:T(8,128)S(1)}, f32[768,512]{1,0:T(8,128)S(1)}, f32[256,512]{1,0:T(8,128)S(1)}) custom-call(f32[256,512]{1,0:T(8,128)S(1)} %copy-done), custom_call_target="tpu_custom_call" | custom-call | tf_op jit(solution)/shard_map/pallas_call | solution.py:418
  73.5 8.4 %shard_map.31 = (f32[256,512]{1,0:T(8,128)}, f32[1024,512]{1,0:T(8,128)}) custom-call(f32[512,256]{1,0:T(8,128)S(1)} %get-tuple-element.5.rest_ref, f32[768,512]{1,0:T(8,128)S(1)} %get-tuple-element.6.top_ref, f32[256,512]{1,0:T(8,128)S(1)} %get-tuple-element.7.first_ref), custom_call_target="tpu_custom_call" | custom-call | tf_op jit(solution)/shard_map/pallas_call | solution.py:482
Async XLA Ops:
  0.6 1.0 %copy-start = (f32[256,512]{1,0:T(8,128)S(1)}, f32[256,512]{1,0:T(8,128)}, u32[]{:S(2)}) copy-start(f32[256,512]{1,0:T(8,128)} %mine_ref.1) | copy-start | bytes 1572868
